TPU v7x, 32 devices: a whole 2x2x4 slice. The times are simulated.
32 devices in a mesh: half: 2 (over core), row: 4 (over y, x), col: 4 (over z).
Axes of the slice: x: 2, y: 2, z: 4, core: 2. Of those that a mesh axis runs over, the one named last changes fastest.
Arguments:
- particles: bfloat16 [64, 2, 64, 4096], P(('half', 'row', 'col')), may hold values from -9 to 9
- orient_bin: int32 [64], P(('half', 'row', 'col')), may hold values from 0 to 15
- tilt_slope: int32 [64, 2], P(('half', 'row', 'col')), may hold values from 12 to 40
- interp_table: bfloat16 [16, 3, 64, 64], replicated, may hold values from 0 to 1.6, as said below
Outputs:
- half_maps: float32 [2, 2, 64, 4096], P('half', None, 'row', 'col')
- shell_power: float32 [2, 29], replicated
- shell_correlation: float32 [2, 29], P('half')
Inputs may be any that keep to these rules, and one draw needn't show every extreme that they name: `interp_table`: nonnegative entries.
All inputs are finite; a program needn't handle non-finite values.
Results may differ from a plain program's by a relative error of at most 0.00063.
Values sent between devices are 32-bit elements; how exact they have to be, the bound alone decides.
A program may use at most 64 MiB of HBM per device.

v0:
```python
import jax
import jax.numpy as jnp
from jax import lax
from jax.sharding import PartitionSpec as P

SHELLS = 29


def partner_2(value, axis, distance):
    mask = 2**distance
    pairs = [(source, source ^ mask) for source in range(lax.axis_size(axis))]
    return lax.ppermute(value, axis, pairs)


def wedge_mask(tilt_limits, grid_size):
    centre = grid_size // 2
    wave_first = (jnp.arange(grid_size, dtype=jnp.int32) - centre)[:, None]
    wave_third = (jnp.arange(grid_size * grid_size, dtype=jnp.int32) % grid_size - centre)[None, :]
    tilt_limit = jnp.where(wave_first * wave_third >= 0, tilt_limits[0], tilt_limits[1])
    inside = 16 * jnp.abs(wave_third) <= tilt_limit * jnp.abs(wave_first)
    return inside.astype(jnp.float32)


def interpolate(stacked, kernels, grid_size):
    components = stacked.shape[0]
    along_first = jnp.einsum(
        "ax,cxm->cam", kernels[0], stacked, preferred_element_type=jnp.float32
    ).astype(jnp.bfloat16)
    along_first = along_first.reshape(components, grid_size, grid_size, grid_size)
    along_second = jnp.einsum(
        "by,cayz->cabz", kernels[1], along_first, preferred_element_type=jnp.float32
    ).astype(jnp.bfloat16)
    along_third = jnp.einsum(
        "dz,cabz->cabd", kernels[2], along_second, preferred_element_type=jnp.float32
    )
    return along_third.reshape(components, grid_size, grid_size * grid_size)


def shell_table(first_index, plane_index, grid_size, shells):
    centre = grid_size // 2
    wave_first = first_index - centre
    wave_second = plane_index // grid_size - centre
    wave_third = plane_index % grid_size - centre
    radius_sq = (
        wave_first * wave_first + wave_second * wave_second + wave_third * wave_third
    ).reshape(-1)
    bounds = jnp.arange(4, centre, dtype=jnp.int32)
    shell_index = jnp.sum(
        (radius_sq[:, None] >= (bounds * bounds)[None, :]).astype(jnp.int32), axis=1
    )
    within = radius_sq < centre * centre
    onehot = (shell_index[:, None] == jnp.arange(shells, dtype=jnp.int32)[None, :]) & within[
        :, None
    ]
    return onehot.astype(jnp.float32)


def spread_slabs(volume):
    slabs = lax.psum_scatter(volume, "row", scatter_dimension=1, tiled=True)
    return lax.psum_scatter(slabs, "col", scatter_dimension=2, tiled=True)


def local(particles, orient_bin, tilt_slope, interp_table):
    grid_size = particles.shape[2]
    particle_count = particles.shape[0]
    rows_local = grid_size // lax.axis_size("row")
    cols_local = grid_size * grid_size // lax.axis_size("col")
    components = 3

    def insert_one(particle, partial_value):
        volume_data = lax.dynamic_index_in_dim(particles, particle, 0, keepdims=False)
        bin_row = lax.dynamic_index_in_dim(orient_bin, particle, 0, keepdims=False)
        tilt_limits = lax.dynamic_index_in_dim(tilt_slope, particle, 0, keepdims=False)
        weight = wedge_mask(tilt_limits, grid_size)
        stacked = jnp.stack([volume_data[0] * weight, volume_data[1] * weight, weight]).astype(
            jnp.bfloat16
        )
        kernels = lax.dynamic_index_in_dim(interp_table, bin_row, 0, keepdims=False)
        return partial_value + interpolate(stacked, kernels, grid_size)

    partial_value = jnp.zeros((components, grid_size, grid_size * grid_size), jnp.float32)
    partial_value = lax.fori_loop(0, particle_count, insert_one, partial_value)
    sums = spread_slabs(partial_value)
    weight_sum = sums[2]
    half_maps = (sums[:2] / (weight_sum[None] + 1.0))[None]
    partner = partner_2(half_maps, "half", 0)
    on_first = lax.axis_index("half") == 0
    map_first = jnp.where(on_first, half_maps, partner)[0]
    map_second = jnp.where(on_first, partner, half_maps)[0]
    cross_term = (map_first[0] * map_second[0] + map_first[1] * map_second[1]).reshape(-1)
    power_first = (map_first[0] * map_first[0] + map_first[1] * map_first[1]).reshape(-1)
    power_second = (map_second[0] * map_second[0] + map_second[1] * map_second[1]).reshape(-1)
    products = jnp.stack([cross_term, power_first, power_second])
    first_index = (
        lax.axis_index("row") * rows_local + jnp.arange(rows_local, dtype=jnp.int32)[:, None]
    )
    plane_index = (
        lax.axis_index("col") * cols_local + jnp.arange(cols_local, dtype=jnp.int32)[None, :]
    )
    onehot = shell_table(first_index, plane_index, grid_size, SHELLS)
    spectra = jnp.dot(products, onehot, precision=lax.Precision.HIGHEST)
    counts = jnp.sum(onehot, axis=0)
    spectra, counts = lax.psum((spectra, counts), ("row", "col"))
    shell_power = spectra[1:3] / counts[None, :]
    shell_correlation = (spectra[0] / jnp.sqrt(spectra[1] * spectra[2] + 1e-06))[None]
    return (half_maps, shell_power, shell_correlation)


def solution(mesh):
    placed = (
        P(("half", "row", "col"), None, None, None),
        P(("half", "row", "col")),
        P(("half", "row", "col"), None),
        P(),
    )
    return jax.shard_map(
        local,
        mesh=mesh,
        in_specs=placed,
        out_specs=(P("half", None, "row", "col"), P(), P("half", None)),
        check_vma=False,
    )
```

profile of v0, /device:TPU:0, one launch (start us, length us, event | category | flops | bytes accessed | tf_op | source)
XLA Modules:
  0.0 190.4 jit_solution(11856617377565038333)
XLA Ops:
  7.2 56.8 %while.17 = (s32[]{:T(128)}, f32[3,64,4096]{2,1,0:T(8,128)}, s32[2,2]{1,0:T(2,128)}, bf16[2,2,64,4096]{3,2,1,0:T(8,128)(2,1)}, s32[2]{0:T(128)}, /*index=5*/bf16...) while((s32[]{:T(128)}, f32[3,64,4096]{2,1,0:T(8,128)}, ...), condition=%wide.region_1.2_spmd.clone, body=%wide.region_0.1_spmd.clone.sunk | while | flops 314609792 | bytes 29511420 | solution.py:82
  8.5 2.9 %fusion.59 = (bf16[1,64,4096]{2,1,0:T(8,128)(2,1)S(1)}, bf16[1,64,4096]{2,1,0:T(8,128)(2,1)S(1)}) fusion(bf16[2,2,64,4096]{3,2,1,0:T(8,128)(2,1)} %get-tuple-element.310, s32[]{:T(128)} %get-tuple-element.296, s32[64]{0:T(128)S(1)} %get-tuple-element.277, s32[]{:T(128)} %bitcast.79, s32[]{:T(128)} %bitcast.80, s32[4096]{0:T(1024)S(1)} %get-tuple-element.280, ...), kind=kLoop, calls=%fused_computation.15.clone.1 | loop fusion | flops 2883584 | bytes 2130448 | tf_op jit(solution)/shard_map/convert.2
  11.4 1.6 convert_convert_fusion.2
  13.0 1.2 dynamic_slice.56
  16.2 2.5 %fusion.60 = bf16[3,64,4096]{2,1,0:T(8,128)(2,1)} fusion(bf16[1,64,4096]{2,1,0:T(8,128)(2,1)S(1)} %convert_convert_fusion.2, bf16[1,64,4096]{2,1,0:T(8,128)(2,1)S(1)} %get-tuple-element.283, bf16[1,64,4096]{2,1,0:T(8,128)(2,1)S(1)} %get-tuple-element.284, bf16[16,3,64,64]{3,2,1,0:T(8,128)(2,1)} %get-tuple-element.312, s32[]{:T(128)S(6)} %select_n.174), kind=kOutput, calls=%fused_computation.1.clone.1 | convolution fusion | flops 106168320 | bytes 3162116 | tf_op jit(solution)/shard_map/while/body/eval_jaxpr/ax,cxm->cam/dot_general | solution.py:26
  18.7 4.3 %reshape.629 = bf16[3,64,64,64]{3,2,1,0:T(8,128)(2,1)S(1)} reshape(bf16[3,64,4096]{2,1,0:T(8,128)(2,1)} %fusion.60) | data formatting | bytes 3145728 | tf_op jit(solution)/shard_map/while/body/eval_jaxpr/reshape | solution.py:29
  23.0 5.2 %fusion.61 = f32[3,64,64,64]{3,2,1,0:T(8,128)} fusion(bf16[3,64,64,64]{3,2,1,0:T(8,128)(2,1)S(1)} %reshape.629, bf16[16,3,64,64]{3,2,1,0:T(8,128)(2,1)} %get-tuple-element.312, s32[]{:T(128)S(6)} %select_n.174, s32[]{:T(128)S(6)} %add.399, s32[]{:T(128)S(6)} %add.397), kind=kOutput, calls=%fused_computation.2.clone.1 | convolution fusion | flops 202113024 | bytes 4753408 | tf_op jit(solution)/shard_map/while/body/eval_jaxpr/dz,cabz->cabd/dot_general | solution.py:33
  28.1 4.5 %reshape.630 = f32[3,64,4096]{2,1,0:T(8,128)S(1)} reshape(f32[3,64,64,64]{3,2,1,0:T(8,128)} %fusion.61) | data formatting | bytes 6291456 | tf_op jit(solution)/shard_map/while/body/eval_jaxpr/reshape | solution.py:36
  32.6 2.1 %select_add_fusion.2 = f32[3,64,4096]{2,1,0:T(8,128)} fusion(f32[3,64,4096]{2,1,0:T(8,128)S(1)} %reshape.630, f32[3,64,4096]{2,1,0:T(8,128)} %get-tuple-element.297, pred[]{:T(512)S(6)} %compare.17), kind=kLoop, calls=%fused_computation.4.clone.1 | loop fusion | flops 1572864 | bytes 9437185 | tf_op jit(solution)/shard_map/while/body/eval_jaxpr/add | solution.py:79
  35.9 2.9 %fusion.59 = (bf16[1,64,4096]{2,1,0:T(8,128)(2,1)S(1)}, bf16[1,64,4096]{2,1,0:T(8,128)(2,1)S(1)}) fusion(bf16[2,2,64,4096]{3,2,1,0:T(8,128)(2,1)} %get-tuple-element.310, s32[]{:T(128)} %get-tuple-element.296, s32[64]{0:T(128)S(1)} %get-tuple-element.277, s32[]{:T(128)} %bitcast.79, s32[]{:T(128)} %bitcast.80, s32[4096]{0:T(1024)S(1)} %get-tuple-element.280, ...), kind=kLoop, calls=%fused_computation.15.clone.1 | loop fusion | flops 2883584 | bytes 2130448 | tf_op jit(solution)/shard_map/convert.2
  38.9 1.6 convert_convert_fusion.2
  40.4 1.2 dynamic_slice.56
  43.6 2.5 %fusion.60 = bf16[3,64,4096]{2,1,0:T(8,128)(2,1)} fusion(bf16[1,64,4096]{2,1,0:T(8,128)(2,1)S(1)} %convert_convert_fusion.2, bf16[1,64,4096]{2,1,0:T(8,128)(2,1)S(1)} %get-tuple-element.283, bf16[1,64,4096]{2,1,0:T(8,128)(2,1)S(1)} %get-tuple-element.284, bf16[16,3,64,64]{3,2,1,0:T(8,128)(2,1)} %get-tuple-element.312, s32[]{:T(128)S(6)} %select_n.174), kind=kOutput, calls=%fused_computation.1.clone.1 | convolution fusion | flops 106168320 | bytes 3162116 | tf_op jit(solution)/shard_map/while/body/eval_jaxpr/ax,cxm->cam/dot_general | solution.py:26
  46.1 4.3 %reshape.629 = bf16[3,64,64,64]{3,2,1,0:T(8,128)(2,1)S(1)} reshape(bf16[3,64,4096]{2,1,0:T(8,128)(2,1)} %fusion.60) | data formatting | bytes 3145728 | tf_op jit(solution)/shard_map/while/body/eval_jaxpr/reshape | solution.py:29
  50.4 5.2 %fusion.61 = f32[3,64,64,64]{3,2,1,0:T(8,128)} fusion(bf16[3,64,64,64]{3,2,1,0:T(8,128)(2,1)S(1)} %reshape.629, bf16[16,3,64,64]{3,2,1,0:T(8,128)(2,1)} %get-tuple-element.312, s32[]{:T(128)S(6)} %select_n.174, s32[]{:T(128)S(6)} %add.399, s32[]{:T(128)S(6)} %add.397), kind=kOutput, calls=%fused_computation.2.clone.1 | convolution fusion | flops 202113024 | bytes 4753408 | tf_op jit(solution)/shard_map/while/body/eval_jaxpr/dz,cabz->cabd/dot_general | solution.py:33
  55.6 4.5 %reshape.630 = f32[3,64,4096]{2,1,0:T(8,128)S(1)} reshape(f32[3,64,64,64]{3,2,1,0:T(8,128)} %fusion.61) | data formatting | bytes 6291456 | tf_op jit(solution)/shard_map/while/body/eval_jaxpr/reshape | solution.py:36
  60.0 4.0 %select_add_fusion.2 = f32[3,64,4096]{2,1,0:T(8,128)} fusion(f32[3,64,4096]{2,1,0:T(8,128)S(1)} %reshape.630, f32[3,64,4096]{2,1,0:T(8,128)} %get-tuple-element.297, pred[]{:T(512)S(6)} %compare.17), kind=kLoop, calls=%fused_computation.4.clone.1 | loop fusion | flops 1572864 | bytes 9437185 | tf_op jit(solution)/shard_map/while/body/eval_jaxpr/add | solution.py:79
  64.1 46.7 %reduce-scatter.3.cloned.1.call-done = f32[3,16,4096]{2,1,0:T(8,128)} async-done(((f32[3,64,4096]{2,1,0:T(8,128)}), f32[3,16,4096]{2,1,0:T(8,128)}) %reduce-scatter.3.cloned.1.call-update) | async-done | bytes 786448 | tf_op jit(solution)/shard_map/reduce_scatter | solution.py:59
  111.4 24.9 %reduce-scatter.5.cloned.1.call-done = f32[3,16,1024]{2,1,0:T(8,128)} async-done(((f32[3,16,4096]{2,1,0:T(8,128)}), f32[3,16,1024]{2,1,0:T(8,128)}) %reduce-scatter.5.cloned.1.call-update) | async-done | bytes 196624 | tf_op jit(solution)/shard_map/reduce_scatter | solution.py:60
  136.3 0.8 fusion.33
  137.1 0.9 fusion.32
  139.5 0.9 broadcast_select_fusion.1
  140.7 1.3 fusion.23
  142.0 40.5 %all-reduce = (f32[3,29]{1,0:T(4,128)S(1)}, f32[29]{0:T(128)S(1)}) all-reduce(f32[3,29]{1,0:T(4,128)S(1)} %fusion.23, f32[29]{0:T(128)S(1)} %convert_reduce_fusion), channel_id=1, replica_groups=mesh['half'=2,'row'=4,'col'=4] {'row','col'}, use_global_device_ids=true, to_apply=%region_5.6 | all-reduce | flops 116 | bytes 928 | tf_op jit(solution)/shard_map/psum | solution.py:103
  (31 shorter events, 6.0 us)
Async XLA Ops:
  7.2 103.6 %reduce-scatter.3.cloned.1.call-start = ((), (), s32[]{:S(2)}) async-start(), calls=%async_computation.2 | async-start | bytes 3932160 | tf_op jit(solution)/shard_map/reduce_scatter | solution.py:59
  64.0 72.3 %reduce-scatter.5.cloned.1.call-start = ((), (), s32[]{:S(2)}) async-start(), calls=%async_computation.3 | async-start | bytes 983040 | tf_op jit(solution)/shard_map/reduce_scatter | solution.py:60
  138.1 45.5 %copy-start = (f32[1,2,16,1024]{3,2,1,0:T(8,128)}, f32[1,2,16,1024]{3,2,1,0:T(8,128)S(1)}, u32[]{:S(2)}) copy-start(f32[1,2,16,1024]{3,2,1,0:T(8,128)S(1)} %fusion.32) | copy-start | bytes 393220
  138.1 1.4 collective-permute-start
Sparse Core Ops, SparseCore 0:
  64.1 46.6 reduce-scatter.2
  113.1 23.1 reduce-scatter.4
where the time goes:
time: 191 us; the launch traced here: 190 us
  waiting for transfers between devices  72.5 us (38%)
  blocking collectives  40.5 us (21%)
  local copies, waits for them, and re-layouts  22.8 us (12%)
  other arithmetic  19.9 us (10%)
  matrix products  16.6 us (9%)
  between operations  14.1 us (7%)
  loops' own time  3.98 us (2%)
    reduce_scatter x1, waiting for transfers between devices, spread_slabs(): slabs = lax.psum_scatter(volume, 'row', scatter_dimension=1, tiled=True)  46.7 us
    psum x1, blocking collectives, local(): spectra, counts = lax.psum((spectra, counts), ('row', 'col'))  40.5 us
    reduce_scatter x1, waiting for transfers between devices, spread_slabs(): return lax.psum_scatter(slabs, 'col', scatter_dimension=2, tiled=True)  24.9 us
    dot_general x2, matrix products, interpolate(): jnp.einsum('dz,cabz->cabd', kernels[2], along_second, preferred_element_t...  10.3 us
    another operation x4, other arithmetic  8.98 us
    reshape x2, local copies, waits for them, and re-layouts, interpolate(): return along_third.reshape(components, grid_size, grid_size * grid_size)  8.9 us
    reshape x2, local copies, waits for them, and re-layouts, interpolate(): along_first.reshape(components, grid_size, grid_size, grid_size)  8.61 us
    add x2, other arithmetic, insert_one(): return partial_value + interpolate(stacked, kernels, grid_size)  6.02 us
  transfers between devices with their start and end apart: 3, of which 3 were waited for; matrix products, arithmetic and copies ran while one was open for 1% of the time, Pallas kernels for 0%

commit v1 on v0

v1 whole, which is shorter than its diff:
```python
import functools

import jax
import jax.numpy as jnp
import numpy as np
from jax import lax
from jax.experimental import pallas as pl
from jax.experimental.pallas import tpu as pltpu
from jax.sharding import PartitionSpec as P

F32 = jnp.float32
BF16 = jnp.bfloat16
LANES = 128
MESH = pl.DeviceIdType.MESH


def dot_nt(left, right):
    return lax.dot_general(left, right, (((1,), (1,)), ((), ())), preferred_element_type=F32)


def dot_nn(left, right):
    return lax.dot_general(left, right, (((1,), (0,)), ((), ())), preferred_element_type=F32)


def block_diagonal(block, copies):
    zero = jnp.zeros_like(block)
    rows = [
        jnp.concatenate([block if i == j else zero for j in range(copies)], axis=1)
        for i in range(copies)
    ]
    return jnp.concatenate(rows, axis=0)


def wedge_mask(limit_same, limit_other, grid, lanes):
    centre = grid // 2
    first = lax.broadcasted_iota(jnp.int32, (grid, lanes), 0) - centre
    third = lax.broadcasted_iota(jnp.int32, (grid, lanes), 1) % grid - centre
    limit = jnp.where(first * third >= 0, limit_same, limit_other)
    inside = 16 * jnp.abs(third) <= limit * jnp.abs(first)
    return jnp.where(inside, 1.0, 0.0).astype(BF16)


def shell_counts(grid):
    centre = grid // 2
    wave = np.arange(grid) - centre
    square = wave * wave
    radius = square[:, None, None] + square[None, :, None] + square[None, None, :]
    shell = np.sum([radius >= k * k for k in range(4, centre)], axis=0)
    return np.bincount(shell[radius < centre * centre], minlength=centre - 3)


def kernel(
    dims,
    bins_ref, tilt_ref, part_ref, table_ref, counts_ref,
    maps_ref, power_ref, corr_ref,
    stage_a, stage_b, sums, rows_in, cols_in, other_map,
    numbers, numbers_in, numbers_s, slab_first, slab_second, weight,
    stats, stats_in, total,
    send_row, recv_row, send_col, recv_col, send_num, recv_num, copy_num,
    send_stat, recv_stat, send_half, recv_half,
):
    grid, particles, R, C, pitch = dims
    N = R * C
    rl, bl = grid // R, grid // C
    cl = bl * grid
    phases = R.bit_length() - 1
    half, row, col = lax.axis_index("half"), lax.axis_index("row"), lax.axis_index("col")
    me = row * C + col

    def peer_id(step):
        peer = (me + step) % N
        return {"row": peer // C, "col": peer % C}

    def power_of(phase):
        low, high = 2 ** (phase % phases), 2 ** ((phase + 1) % phases)
        return low + half * (high - low)

    def row_partner(phase):
        weight_of = power_of(phase)
        bit = (row // weight_of) % 2
        return {"row": row + (1 - 2 * bit) * weight_of}

    def slab_of(index):
        slab = row
        for phase in range(phases):
            if (index >> (phases - 1 - phase)) & 1:
                weight_of = power_of(phase)
                bit = (row // weight_of) % 2
                slab = slab + (1 - 2 * bit) * weight_of
        return slab

    barrier = pltpu.get_barrier_semaphore()
    for step in range(1, N):
        pl.semaphore_signal(barrier, inc=1, device_id=peer_id(step), device_id_type=MESH)
    pl.semaphore_signal(barrier, inc=1, device_id={"half": 1 - half}, device_id_type=MESH)

    lane = lax.broadcasted_iota(jnp.int32, (1, LANES), 1)
    packed = jnp.zeros((1, LANES), jnp.int32)
    for p in range(particles):
        for i, value in enumerate((bins_ref[p], tilt_ref[p, 0], tilt_ref[p, 1])):
            packed = jnp.where(lane == 3 * p + i, value, packed)
    numbers[0] = packed
    numbers_in[me] = packed

    tiles = 4
    width = tiles * LANES
    seconds = width // grid

    for p in range(particles):
        bin_row = bins_ref[p]
        first = table_ref[bin_row, 0].astype(F32)
        second = table_ref[bin_row, 1].astype(F32)
        for r in range(R):
            slab_first[p, r] = first[r * rl:(r + 1) * rl]
        for q in range(C):
            slab_second[p, q] = second[q * bl:(q + 1) * bl]
        first = jnp.concatenate([slab_first[p, slab_of(j)] for j in range(R)], axis=0).astype(BF16)
        second = jnp.concatenate(
            [slab_second[p, (col + 1 + k) % C] for k in range(C)], axis=0
        ).astype(BF16)
        first = block_diagonal(first, 2)
        mask = wedge_mask(tilt_ref[p, 0], tilt_ref[p, 1], grid, LANES)
        mask = jnp.concatenate([mask] * tiles, axis=1)
        mask = jnp.concatenate([mask, mask], axis=0)

        def along_first(step, carry):
            span = pl.ds(pl.multiple_of(step * width, width), width)
            block = jnp.concatenate([part_ref[p, 0, :, span], part_ref[p, 1, :, span]], axis=0)
            result = dot_nt((block * mask).T, first)
            for i in range(seconds):
                at = pl.multiple_of((step * seconds + i) * pitch, 8)
                stage_a[pl.ds(at, grid), :] = result[i * grid:(i + 1) * grid]
            return carry

        lax.fori_loop(0, grid * grid // width, along_first, 0, unroll=2)

        for z in range(0, grid, 2):
            block = jnp.concatenate(
                [stage_a[pl.ds(z + i, grid, stride=pitch), :] for i in range(2)], axis=1
            ).astype(BF16)
            result = dot_nn(second, block)
            for i in range(2):
                stage_b[p, pl.ds((z + i) * pitch, grid), :] = result[:, i * LANES:(i + 1) * LANES]

    pl.semaphore_wait(barrier, N)

    num_copies = [
        pltpu.make_async_remote_copy(
            src_ref=numbers.at[0], dst_ref=numbers_in.at[me],
            send_sem=send_num.at[step - 1], recv_sem=recv_num.at[step - 1],
            device_id=peer_id(step), device_id_type=MESH,
        )
        for step in range(1, N)
    ]
    for copy in num_copies:
        copy.start()

    def row_copy(phase, k):
        keep = R >> (phase + 1)
        return pltpu.make_async_remote_copy(
            src_ref=sums.at[k, pl.ds(keep, keep)],
            dst_ref=rows_in.at[k, pl.ds(keep, keep)],
            send_sem=send_row.at[phase, k], recv_sem=recv_row.at[phase, k],
            device_id=row_partner(phase), device_id_type=MESH,
        )

    def col_copy(k):
        return pltpu.make_async_remote_copy(
            src_ref=sums.at[k, 0], dst_ref=cols_in.at[k],
            send_sem=send_col.at[k], recv_sem=recv_col.at[k],
            device_id={"col": (col + 1 + k) % C}, device_id_type=MESH,
        )

    third = jnp.concatenate(
        [block_diagonal(table_ref[bins_ref[p], 2], 2) for p in range(particles)], axis=1
    )
    for k in range(C):
        for pair in range(bl // 2):
            at = k * bl + 2 * pair
            block = jnp.concatenate(
                [
                    stage_b[p, pl.ds(at + i, grid, stride=pitch), :]
                    for p in range(particles)
                    for i in range(2)
                ],
                axis=0,
            ).astype(BF16)
            result = dot_nt(block.T, third)
            for j in range(R):
                for c in range(2):
                    sums[k, j, c, :, pair * LANES:(pair + 1) * LANES] = result[
                        c * grid + j * rl:c * grid + (j + 1) * rl
                    ]
        row_copy(0, k).start()

    for copy in num_copies:
        copy.wait_recv()
    local = pltpu.make_async_copy(numbers_in, numbers_s, copy_num)
    local.start()
    local.wait()
    weight[...] = jnp.zeros_like(weight)
    ones = jnp.ones((grid, grid), BF16)

    def add_weight(n, carry):
        firsts, seconds_, thirds = [], [], []
        for p in range(particles):
            bin_row = numbers_s[n, 0, 3 * p]
            mask = wedge_mask(numbers_s[n, 0, 3 * p + 1], numbers_s[n, 0, 3 * p + 2], grid, grid)
            first = dot_nn(table_ref[bin_row, 0], mask)
            second = dot_nn(table_ref[bin_row, 1], ones)
            for r in range(R):
                slab_first[p, r] = first[r * rl:(r + 1) * rl]
            for q in range(C):
                slab_second[p, q] = second[q * bl:(q + 1) * bl]
            firsts.append(slab_first[p, row])
            seconds_.append(slab_second[p, col])
            thirds.append(table_ref[bin_row, 2])
        first = jnp.concatenate(firsts, axis=1).astype(BF16).astype(F32)
        second = jnp.concatenate(seconds_, axis=1)
        third_ = jnp.concatenate(thirds, axis=1)
        block = jnp.concatenate([first * second[b:b + 1] for b in range(bl)], axis=0)
        weight[...] += dot_nt(block.astype(BF16), third_)
        return carry

    share = N // C
    for step in range(C + phases):
        if step < C:
            lax.fori_loop(step * share, (step + 1) * share, add_weight, 0)
        for phase in range(phases):
            k = step - phase
            if 0 <= k < C:
                keep = R >> (phase + 1)
                row_copy(phase, k).wait_recv()
                sums[k, :keep] = sums[k, :keep] + rows_in[k, keep:2 * keep]
                if phase + 1 < phases:
                    row_copy(phase + 1, k).start()
                elif k < C - 1:
                    col_copy(k).start()

    for k in range(C - 1):
        col_copy(k).wait_recv()
    for pair in range(bl // 2):
        span = slice(pair * LANES, (pair + 1) * LANES)
        low = 2 * pair * rl
        below = jnp.concatenate(
            [weight[low:low + rl], weight[low + rl:low + 2 * rl]], axis=1
        ) + 1.0
        for c in range(2):
            above = sums[C - 1, 0, c, :, span]
            for k in range(C - 1):
                above = above + cols_in[k, c, :, span]
            maps_ref[0, c, :, span] = above / below

    half_copy = pltpu.make_async_remote_copy(
        src_ref=maps_ref.at[0], dst_ref=other_map, send_sem=send_half, recv_sem=recv_half,
        device_id={"half": 1 - half}, device_id_type=MESH,
    )
    half_copy.start()
    for k in range(C):
        for phase in range(phases):
            row_copy(phase, k).wait_send()
    for k in range(C - 1):
        col_copy(k).wait_send()
    for copy in num_copies:
        copy.wait_send()
    half_copy.wait()

    centre = grid // 2
    shells = centre - 3
    tile_rows = lax.broadcasted_iota(jnp.int32, (rl, LANES), 0)
    tile_lanes = lax.broadcasted_iota(jnp.int32, (rl, LANES), 1)
    wave_first = row * rl + tile_rows - centre
    wave_third = tile_lanes % grid - centre
    on_first = (1 - half).astype(F32)
    on_second = half.astype(F32)
    fixed = wave_first * wave_first + wave_third * wave_third
    radius, products = [], []
    for pair in range(bl // 2):
        span = slice(pair * LANES, (pair + 1) * LANES)
        wave_second = col * bl + 2 * pair + tile_lanes // grid - centre
        radius.append(fixed + wave_second * wave_second)
        mine = [maps_ref[0, c, :, span] for c in range(2)]
        theirs = [other_map[c, :, span] for c in range(2)]
        own = mine[0] * mine[0] + mine[1] * mine[1]
        far = theirs[0] * theirs[0] + theirs[1] * theirs[1]
        products.append((
            mine[0] * theirs[0] + mine[1] * theirs[1],
            on_first * own + on_second * far,
            on_first * far + on_second * own,
        ))
    stats[...] = jnp.zeros_like(stats)
    for s in range(shells):
        least = (s + 3) * (s + 3) if s else 0
        beyond = (s + 4) * (s + 4)
        parts = [jnp.zeros((rl, LANES), F32) for _ in range(3)]
        for r2, values in zip(radius, products):
            inside = (r2 >= least) & (r2 < beyond)
            parts = [part + jnp.where(inside, value, 0.0) for part, value in zip(parts, values)]
        for i in range(3):
            stats[i * 32 + s:i * 32 + s + 1, :] = jnp.sum(parts[i], axis=0, keepdims=True)
    mine = jnp.sum(stats[...].T, axis=0, keepdims=True)
    total[0] = mine
    stats_in[me] = mine
    stat_copies = [
        pltpu.make_async_remote_copy(
            src_ref=total.at[0], dst_ref=stats_in.at[me],
            send_sem=send_stat.at[step - 1], recv_sem=recv_stat.at[step - 1],
            device_id=peer_id(step), device_id_type=MESH,
        )
        for step in range(1, N)
    ]
    for copy in stat_copies:
        copy.start()
    for copy in stat_copies:
        copy.wait()
    spectra = stats_in[0]
    for n in range(1, N):
        spectra = spectra + stats_in[n]
    cross = spectra[:, 0:shells]
    power_first = spectra[:, 32:32 + shells]
    power_second = spectra[:, 64:64 + shells]
    power_ref[0:1, :] = power_first / counts_ref[...]
    power_ref[1:2, :] = power_second / counts_ref[...]
    corr_ref[...] = cross / jnp.sqrt(power_first * power_second + 1e-6)


def solution(mesh):
    R, C = mesh.shape["row"], mesh.shape["col"]
    N = R * C

    def local(particles, orient_bin, tilt_slope, interp_table):
        count, _, grid, plane = particles.shape
        rl, cl, bl = grid // R, plane // C, grid // C
        shells = grid // 2 - 3
        phases = R.bit_length() - 1
        pitch = grid + 8
        counts = jnp.asarray(shell_counts(grid)[None], F32)
        vmem, smem = pl.BlockSpec(memory_space=pltpu.VMEM), pl.BlockSpec(memory_space=pltpu.SMEM)
        dma = pltpu.SemaphoreType.DMA
        return pl.pallas_call(
            functools.partial(kernel, (grid, count, R, C, pitch)),
            out_shape=(
                jax.ShapeDtypeStruct((1, 2, rl, cl), F32),
                jax.ShapeDtypeStruct((2, shells), F32),
                jax.ShapeDtypeStruct((1, shells), F32),
            ),
            in_specs=[smem, smem, vmem, vmem, vmem],
            out_specs=(vmem, vmem, vmem),
            scratch_shapes=[
                pltpu.VMEM((grid * pitch, LANES), F32),
                pltpu.VMEM((count, grid * pitch, LANES), F32),
                pltpu.VMEM((C, R, 2, rl, cl), F32),
                pltpu.VMEM((C, R, 2, rl, cl), F32),
                pltpu.VMEM((C - 1, 2, rl, cl), F32),
                pltpu.VMEM((2, rl, cl), F32),
                pltpu.VMEM((1, 1, LANES), jnp.int32),
                pltpu.VMEM((N, 1, LANES), jnp.int32),
                pltpu.SMEM((N, 1, LANES), jnp.int32),
                pltpu.VMEM((count, R, rl, grid), F32),
                pltpu.VMEM((count, C, bl, grid), F32),
                pltpu.VMEM((bl * rl, grid), F32),
                pltpu.VMEM((LANES, LANES), F32),
                pltpu.VMEM((N, 1, LANES), F32),
                pltpu.VMEM((1, 1, LANES), F32),
                dma((phases, C)), dma((phases, C)),
                dma((C - 1,)), dma((C - 1,)),
                dma((N - 1,)), dma((N - 1,)), dma,
                dma((N - 1,)), dma((N - 1,)),
                dma, dma,
            ],
            compiler_params=pltpu.CompilerParams(
                collective_id=0, has_side_effects=True, vmem_limit_bytes=56 * 1024 * 1024
            ),
        )(orient_bin, tilt_slope, particles, interp_table, counts)

    placed = (
        P(("half", "row", "col"), None, None, None),
        P(("half", "row", "col")),
        P(("half", "row", "col"), None),
        P(),
    )
    return jax.shard_map(
        local,
        mesh=mesh,
        in_specs=placed,
        out_specs=(P("half", None, "row", "col"), P(), P("half", None)),
        check_vma=False,
    )
```

time: 191 us -> 45.9 us (0.24)
  waiting for transfers between devices: 72.5 us -> 0 us
  Pallas kernels: 0 us -> 41.1 us
  blocking collectives: 40.5 us -> 0 us
  other arithmetic: 19.9 us -> 0 us
  local copies, waits for them, and re-layouts: 22.8 us -> 3.96 us
  matrix products: 16.6 us -> 0 us
  between operations: 14.1 us -> 0.64 us
  loops' own time: 3.98 us -> 0 us
    reduce_scatter x2 -> x0, waiting for transfers between devices: 71.6 us -> none  [the longest x1 46.7 us: spread_slabs(): slabs = lax.psum_scatter(volume, 'row', scatter_dimension=1, tiled=True)]
    pallas_call x0 -> x1, Pallas kernels: none -> 41.1 us  [local(): pl.pallas_call(functools.partial(kernel, (grid, count, R, C, pitch)), out...]
    psum x1 -> x0, blocking collectives: 40.5 us -> none  [local(): spectra, counts = lax.psum((spectra, counts), ('row', 'col'))]
    reshape x4 -> x0, local copies, waits for them, and re-layouts: 17.5 us -> none  [the longest x2 8.9 us: interpolate(): return along_third.reshape(components, grid_size, grid_size * grid_size)]
    dot_general x5 -> x0, matrix products: 16.6 us -> none  [the longest x2 10.3 us: interpolate(): jnp.einsum('dz,cabz->cabd', kernels[2], along_second, preferred_element_t...]
    another operation x4 -> x0, other arithmetic: 8.98 us -> none
    add x2 -> x0, other arithmetic: 6.02 us -> none  [insert_one(): return partial_value + interpolate(stacked, kernels, grid_size)]
    another operation x1 -> x0, loops' own time: 3.98 us -> none  [local(): partial_value = lax.fori_loop(0, particle_count, insert_one, partial_value)]
  transfers between devices with their start and end apart: 3 -> 0, of which waited for: 3 -> 0; matrix products, arithmetic and copies ran while one was open for 1% -> 0% of each run, Pallas kernels for 0% -> 0%
where the time goes in v1:
time: 45.9 us; the launch traced here: 45.7 us
  Pallas kernels  41.1 us (90%)
  local copies, waits for them, and re-layouts  3.96 us (9%)
  between operations  0.64 us (1%)
    pallas_call x1, Pallas kernels, local(): pl.pallas_call(functools.partial(kernel, (grid, count, R, C, pitch)), out...  41.1 us
    unnamed x3, local copies, waits for them, and re-layouts  3.96 us

profile of v1, /device:TPU:0, one launch (start us, length us, event | category | flops | bytes accessed | tf_op | source)
XLA Modules:
  0.0 45.7 jit_solution(9028469312743959945)
XLA Ops:
  0.6 41.1 %shard_map.76 = (f32[1,2,16,1024]{3,2,1,0:T(8,128)}, f32[2,29]{1,0:T(2,128)}, f32[1,29]{1,0:T(1,128)}) custom-call(s32[2]{0:T(128)} %bins_ref.1, s32[2,2]{1,0:T(2,128)} %tilt_ref.1, bf16[2,2,64,4096]{3,2,1,0:T(8,128)(2,1)} %part_ref.1, bf16[16,3,64,64]{3,2,1,0:T(8,128)(2,1)} %table_ref.1, f32[1,29]{1,0:T(1,128)} %constant.2.clone.counts_ref), custom_call_target="tpu_custom_call" | custom-call | tf_op jit(solution)/shard_map/pallas_call | solution.py:340
  41.7 1.6 %copy.11 = f32[1,2,16,1024]{3,2,1,0:T(8,128)} copy(f32[1,2,16,1024]{3,2,1,0:T(8,128)} %get-tuple-element.6) | data formatting | bytes 262144
  43.3 1.2 %copy.12 = f32[2,29]{1,0:T(2,128)} copy(f32[2,29]{1,0:T(2,128)} %get-tuple-element.7) | data formatting | bytes 464
  44.5 1.2 %copy.13 = f32[1,29]{1,0:T(1,128)} copy(f32[1,29]{1,0:T(1,128)} %get-tuple-element.8) | data formatting | bytes 232

commit v2 on v1

--- a/solution.py
+++ b/solution.py
@@ -51,13 +51,13 @@
 
 def kernel(
     dims,
-    bins_ref, tilt_ref, part_ref, table_ref, counts_ref,
-    maps_ref, power_ref, corr_ref,
-    stage_a, stage_b, sums, rows_in, cols_in, other_map,
+    bins_ref, tilt_ref, part_hbm, table_hbm,
+    maps_ref, spectra_ref,
+    part_ref, table_ref, stage_a, stage_b, sums, rows_in, cols_in, other_map,
     numbers, numbers_in, numbers_s, slab_first, slab_second, weight,
     stats, stats_in, total,
     send_row, recv_row, send_col, recv_col, send_num, recv_num, copy_num,
-    send_stat, recv_stat, send_half, recv_half,
+    send_stat, recv_stat, send_half, recv_half, load_part, load_table,
 ):
     grid, particles, R, C, pitch = dims
     N = R * C
@@ -89,6 +89,15 @@
                 slab = slab + (1 - 2 * bit) * weight_of
         return slab
 
+    table_load = pltpu.make_async_copy(table_hbm, table_ref, load_table)
+    table_load.start()
+    part_loads = [
+        pltpu.make_async_copy(part_hbm.at[p], part_ref.at[p], load_part.at[p])
+        for p in range(particles)
+    ]
+    for copy in part_loads:
+        copy.start()
+
     barrier = pltpu.get_barrier_semaphore()
     for step in range(1, N):
         pl.semaphore_signal(barrier, inc=1, device_id=peer_id(step), device_id_type=MESH)
@@ -106,6 +115,7 @@
     width = tiles * LANES
     seconds = width // grid
 
+    table_load.wait()
     for p in range(particles):
         bin_row = bins_ref[p]
         first = table_ref[bin_row, 0].astype(F32)
@@ -132,6 +142,7 @@
                 stage_a[pl.ds(at, grid), :] = result[i * grid:(i + 1) * grid]
             return carry
 
+        part_loads[p].wait()
         lax.fori_loop(0, grid * grid // width, along_first, 0, unroll=2)
 
         for z in range(0, grid, 2):
@@ -316,6 +327,12 @@
     spectra = stats_in[0]
     for n in range(1, N):
         spectra = spectra + stats_in[n]
+    spectra_ref[...] = spectra
+
+
+def finish(shells, maps_in_ref, spectra_ref, counts_ref, maps_ref, power_ref, corr_ref):
+    maps_ref[...] = maps_in_ref[...]
+    spectra = spectra_ref[...]
     cross = spectra[:, 0:shells]
     power_first = spectra[:, 32:32 + shells]
     power_second = spectra[:, 64:64 + shells]
@@ -336,17 +353,19 @@
         pitch = grid + 8
         counts = jnp.asarray(shell_counts(grid)[None], F32)
         vmem, smem = pl.BlockSpec(memory_space=pltpu.VMEM), pl.BlockSpec(memory_space=pltpu.SMEM)
+        anywhere = pl.BlockSpec(memory_space=pl.ANY)
         dma = pltpu.SemaphoreType.DMA
-        return pl.pallas_call(
+        maps, spectra = pl.pallas_call(
             functools.partial(kernel, (grid, count, R, C, pitch)),
             out_shape=(
                 jax.ShapeDtypeStruct((1, 2, rl, cl), F32),
-                jax.ShapeDtypeStruct((2, shells), F32),
-                jax.ShapeDtypeStruct((1, shells), F32),
+                jax.ShapeDtypeStruct((1, LANES), F32),
             ),
-            in_specs=[smem, smem, vmem, vmem, vmem],
-            out_specs=(vmem, vmem, vmem),
+            in_specs=[smem, smem, anywhere, anywhere],
+            out_specs=(vmem, vmem),
             scratch_shapes=[
+                pltpu.VMEM(particles.shape, particles.dtype),
+                pltpu.VMEM(interp_table.shape, interp_table.dtype),
                 pltpu.VMEM((grid * pitch, LANES), F32),
                 pltpu.VMEM((count, grid * pitch, LANES), F32),
                 pltpu.VMEM((C, R, 2, rl, cl), F32),
@@ -366,12 +385,22 @@
                 dma((C - 1,)), dma((C - 1,)),
                 dma((N - 1,)), dma((N - 1,)), dma,
                 dma((N - 1,)), dma((N - 1,)),
-                dma, dma,
+                dma, dma, dma((count,)), dma,
             ],
             compiler_params=pltpu.CompilerParams(
                 collective_id=0, has_side_effects=True, vmem_limit_bytes=56 * 1024 * 1024
             ),
-        )(orient_bin, tilt_slope, particles, interp_table, counts)
+        )(orient_bin, tilt_slope, particles, interp_table)
+        return pl.pallas_call(
+            functools.partial(finish, shells),
+            out_shape=(
+                jax.ShapeDtypeStruct((1, 2, rl, cl), F32),
+                jax.ShapeDtypeStruct((2, shells), F32),
+                jax.ShapeDtypeStruct((1, shells), F32),
+            ),
+            in_specs=[vmem, vmem, vmem],
+            out_specs=(vmem, vmem, vmem),
+        )(maps, spectra, counts)
 
     placed = (
         P(("half", "row", "col"), None, None, None),

time: 45.9 us -> 43.5 us (0.948)
  local copies, waits for them, and re-layouts: 3.96 us -> 0 us
  Pallas kernels: 41.1 us -> 42.6 us
    unnamed x3 -> x0, local copies, waits for them, and re-layouts: 3.96 us -> none
    pallas_call x0 -> x1, Pallas kernels: none -> 1.63 us  [local(): pl.pallas_call(functools.partial(finish, shells), out_shape=(jax.ShapeDty...]
where the time goes in v2:
time: 43.5 us; the launch traced here: 43.3 us
  Pallas kernels  42.6 us (98%)
  between operations  0.64 us (1%)
    pallas_call x1, Pallas kernels, local(): pl.pallas_call(functools.partial(kernel, (grid, count, R, C, pitch)), out...  41 us
    pallas_call x1, Pallas kernels, local(): pl.pallas_call(functools.partial(finish, shells), out_shape=(jax.ShapeDty...  1.63 us

profile of v2, /device:TPU:0, one launch (start us, length us, event | category | flops | bytes accessed | tf_op | source)
XLA Modules:
  0.0 43.3 jit_solution(3297986007963984402)
XLA Ops:
  0.6 41.0 %shard_map.76 = (f32[1,2,16,1024]{3,2,1,0:T(8,128)}, f32[1,128]{1,0:T(1,128)}) custom-call(s32[2]{0:T(128)} %bins_ref.1, s32[2,2]{1,0:T(2,128)} %tilt_ref.1, bf16[2,2,64,4096]{3,2,1,0:T(8,128)(2,1)} %part_hbm.1, bf16[16,3,64,64]{3,2,1,0:T(8,128)(2,1)} %table_hbm.1), custom_call_target="tpu_custom_call" | custom-call | tf_op jit(solution)/shard_map/pallas_call | solution.py:358
  41.6 1.6 %shard_map.77 = (f32[1,2,16,1024]{3,2,1,0:T(8,128)}, f32[2,29]{1,0:T(2,128)}, f32[1,29]{1,0:T(1,128)}) custom-call(f32[1,2,16,1024]{3,2,1,0:T(8,128)} %get-tuple-element.5.maps_in_ref, f32[1,128]{1,0:T(1,128)} %get-tuple-element.6.spectra_ref, f32[1,29]{1,0:T(1,128)} %constant.2.clone.counts_ref), custom_call_target="tpu_custom_call" | custom-call | tf_op jit(solution)/shard_map/pallas_call | solution.py:394

commit v3 on v2

--- a/solution.py
+++ b/solution.py
@@ -204,11 +204,7 @@
                     ]
         row_copy(0, k).start()
 
-    for copy in num_copies:
-        copy.wait_recv()
     local = pltpu.make_async_copy(numbers_in, numbers_s, copy_num)
-    local.start()
-    local.wait()
     weight[...] = jnp.zeros_like(weight)
     ones = jnp.ones((grid, grid), BF16)
 
@@ -235,8 +231,6 @@
 
     share = N // C
     for step in range(C + phases):
-        if step < C:
-            lax.fori_loop(step * share, (step + 1) * share, add_weight, 0)
         for phase in range(phases):
             k = step - phase
             if 0 <= k < C:
@@ -247,6 +241,13 @@
                     row_copy(phase + 1, k).start()
                 elif k < C - 1:
                     col_copy(k).start()
+        if step == 0:
+            for copy in num_copies:
+                copy.wait_recv()
+            local.start()
+            local.wait()
+        if step < C:
+            lax.fori_loop(step * share, (step + 1) * share, add_weight, 0)
 
     for k in range(C - 1):
         col_copy(k).wait_recv()

time: 43.5 us -> 41.9 us (0.963)
  Pallas kernels: 42.6 us -> 41.1 us
    pallas_call x1, Pallas kernels: 41 us -> 39.5 us  [local(): pl.pallas_call(functools.partial(kernel, (grid, count, R, C, pitch)), out...]
where the time goes in v3:
time: 41.9 us; the launch traced here: 41.8 us
  Pallas kernels  41.1 us (98%)
  between operations  0.64 us (2%)
    pallas_call x1, Pallas kernels, local(): pl.pallas_call(functools.partial(kernel, (grid, count, R, C, pitch)), out...  39.5 us
    pallas_call x1, Pallas kernels, local(): pl.pallas_call(functools.partial(finish, shells), out_shape=(jax.ShapeDty...  1.63 us

profile of v3, /device:TPU:0, one launch (start us, length us, event | category | flops | bytes accessed | tf_op | source)
XLA Modules:
  0.0 41.8 jit_solution(8747429594528675477)
XLA Ops:
  0.6 39.5 %shard_map.76 = (f32[1,2,16,1024]{3,2,1,0:T(8,128)}, f32[1,128]{1,0:T(1,128)}) custom-call(s32[2]{0:T(128)} %bins_ref.1, s32[2,2]{1,0:T(2,128)} %tilt_ref.1, bf16[2,2,64,4096]{3,2,1,0:T(8,128)(2,1)} %part_hbm.1, bf16[16,3,64,64]{3,2,1,0:T(8,128)(2,1)} %table_hbm.1), custom_call_target="tpu_custom_call" | custom-call | tf_op jit(solution)/shard_map/pallas_call | solution.py:359
  40.1 1.6 %shard_map.77 = (f32[1,2,16,1024]{3,2,1,0:T(8,128)}, f32[2,29]{1,0:T(2,128)}, f32[1,29]{1,0:T(1,128)}) custom-call(f32[1,2,16,1024]{3,2,1,0:T(8,128)} %get-tuple-element.5.maps_in_ref, f32[1,128]{1,0:T(1,128)} %get-tuple-element.6.spectra_ref, f32[1,29]{1,0:T(1,128)} %constant.2.clone.counts_ref), custom_call_target="tpu_custom_call" | custom-call | tf_op jit(solution)/shard_map/pallas_call | solution.py:395
